TPU v7x, 32 devices: a 4x4x1 block of a 4x4x8 slice. The times are simulated.
32 devices in a mesh: batch: 1 (over z), row: 4 (over y), col: 8 (over x, core).
Axes of the slice: x: 4, y: 4, z: 1, core: 2. Of those that a mesh axis runs over, the one named last changes fastest.
The devices are a block of a 4x4x8 slice.
Arguments:
- spd_blocks: float32 [32, 256, 8192], P(('batch', 'row'), None, 'col')
Outputs:
- output: float32 [32, 256, 8192], P(('batch', 'row'), None, 'col')
All inputs are finite; a program needn't handle non-finite values.
Results may differ from a plain program's by a relative error of at most 0.001.
Values are sent between devices in bfloat16 or wider.
A program may use at most 768 MiB of HBM per device.

v0:
```python
import functools

import jax
import jax.numpy as jnp
from jax import lax
from jax.experimental import pallas as pl
from jax.experimental.pallas import tpu as pltpu
from jax.sharding import PartitionSpec as P

F32 = jnp.float32
BF16 = jnp.bfloat16
MESH = pl.DeviceIdType.MESH
SUB = 8
LANE = 128
BASE = 16
LEAD = 1
SETTLE = 3
LAG = 3


def sub_bcast(x, q):
    return jnp.broadcast_to(x[q : q + 1, :], (SUB, LANE))


ALONG_LANES = lax.GatherDimensionNumbers(
    offset_dims=(), collapsed_slice_dims=(1,), start_index_map=(1,), operand_batching_dims=(0,), start_indices_batching_dims=(0,)
)


def lane_bcast(x, lane):
    index = jnp.full((SUB, LANE, 1), lane, jnp.int32)
    return lax.gather(x, index, ALONG_LANES, (1, 1), mode=lax.GatherScatterMode.PROMISE_IN_BOUNDS)


def split3(x):
    high = x.astype(BF16)
    rest = x - high.astype(F32)
    mid = rest.astype(BF16)
    return high, mid, (rest - mid.astype(F32)).astype(BF16)


def swap_rows(x, bit, row_id):
    if bit == SUB // 2:
        return pltpu.roll(x, bit, 0)
    return jnp.where((row_id & bit) == 0, pltpu.roll(x, SUB - bit, 0), pltpu.roll(x, bit, 0))


def stack_sums(parts):
    row_id = lax.broadcasted_iota(jnp.int32, (SUB, LANE), 0)
    for bit in (4, 2, 1):
        low = (row_id & bit) == 0
        half = len(parts) // 2
        parts = [
            jnp.where(low, parts[n], parts[n + half]) + swap_rows(jnp.where(low, parts[n + half], parts[n]), bit, row_id)
            for n in range(half)
        ]
    return parts[0]


def eliminate(rows, lane0):
    row_id = lax.broadcasted_iota(jnp.int32, (SUB, LANE), 0)
    rows = [list(rows[0]), list(rows[1])]
    cols = [
        [lane_bcast(rows[0][0], lane0 + j) for j in range(SUB)],
        [lane_bcast(rows[1][0], lane0 + j) for j in range(BASE)],
    ]
    scale = [jnp.zeros((SUB, LANE), F32), jnp.zeros((SUB, LANE), F32)]
    pivot = sub_bcast(cols[0][0], 0)
    for j in range(BASE):
        t, q = divmod(j, SUB)
        inv = lax.rsqrt(pivot)
        scale[t] = jnp.where(row_id == q, inv, scale[t])
        if j + 1 < BASE:
            tn, qn = divmod(j + 1, SUB)
            near = sub_bcast(cols[tn][j], qn) * inv
            pivot = sub_bcast(cols[tn][j + 1], qn) - near * near
        below = cols[1][j] * inv
        here = cols[0][j] * inv if t == 0 else None
        for n in range(j + 1, BASE):
            tn, qn = divmod(n, SUB)
            other = near if n == j + 1 else sub_bcast(here if tn == 0 else below, qn)
            if t == 0 and tn == 0:
                cols[0][n] = cols[0][n] - here * other
            cols[1][n] = cols[1][n] - below * other
        masked = jnp.where(row_id > q, here if t == 0 else below, 0.0)
        for v in range(len(rows[0])):
            pivot_row = sub_bcast(rows[t][v], q) * inv
            rows[t][v] = rows[t][v] - masked * pivot_row
            if t == 0:
                rows[1][v] = rows[1][v] - below * pivot_row
    return [[x * scale[t] for x in rows[t]] for t in range(2)]


def factor_block(work, winv, winv3, prev, fac):
    size = work.shape[1]

    def group(v):
        return slice(LANE * v, LANE * (v + 1))

    def pending(factors, before, t, v):
        above, below = before[:SUB, group(v)], before[SUB:, group(v)]
        at = 2 * SUB * t
        return stack_sums([factors[at + n] * above + factors[at + SUB + n] * below for n in range(SUB)])

    for half in range(size // LANE):
        views = [(work, 0), (work, 1), (winv, 0)] if half == 0 else [(work, 1), (winv, 0), (winv, 1)]
        first = half * LANE
        if half == 1:
            factors, before = fac[...], prev[...]
            work[first : first + BASE, group(1)] -= jnp.concatenate([pending(factors, before, t, 1) for t in range(2)], axis=0)
            prev[...] = jnp.concatenate([before[:, group(1)], before[:, group(2)], jnp.zeros((BASE, LANE), F32)], axis=1)

        def body(s, carry, views=views, first=first):
            lane0 = s * BASE
            row0 = pl.multiple_of(first + lane0, BASE)

            here = pl.ds(row0, BASE)
            then = pl.ds(pl.multiple_of(row0 + BASE, BASE), BASE)
            both = [ref[here, group(g)] for ref, g in views]
            rows = [[x[SUB * t : SUB * (t + 1)] for x in both] for t in range(2)]
            factors, before = fac[...], prev[...]
            for t in range(2):
                for v in (1, 2):
                    rows[t][v] = rows[t][v] - pending(factors, before, t, v)
            hi, mid, lo = split3(before)
            lane = lax.broadcasted_iota(jnp.int32, (BASE, size - first), 1) + first
            after = lane >= row0 + BASE
            lhi, lmid, llo = [jnp.where(after, x[:, : size - first], jnp.zeros((), BF16)) for x in (hi, mid, lo)]
            update = lax.dot_general(
                jnp.concatenate([lhi, lhi, lmid, lhi, llo, lmid], axis=0),
                jnp.concatenate([hi, mid, hi, lo, hi, mid], axis=0),
                (((0,), (0,)), ((), ())),
                preferred_element_type=F32,
            )
            for v, (ref, g) in enumerate(views):
                ref[first:size, group(g)] -= update[:, group(v)]
            done = eliminate(rows, lane0)
            if first == 0:
                source = [jnp.where(s == LANE // BASE - 1, done[t][1], done[t][0]) for t in range(2)]
            else:
                source = [done[t][0] for t in range(2)]
            next_lane = (lane0 + BASE) % LANE
            factors, sums = [], []
            for t in range(2):
                factor = [[lane_bcast(source[m], next_lane + SUB * t + n) for n in range(SUB)] for m in range(2)]
                sums.append(stack_sums([factor[0][n] * done[0][0] + factor[1][n] * done[1][0] for n in range(SUB)]))
                factors += factor[0] + factor[1]
            ref, g = views[0]
            ref[then, group(g)] -= jnp.concatenate(sums, axis=0)
            fac[...] = jnp.stack(factors)
            whole = [jnp.concatenate([done[0][v], done[1][v]], axis=0) for v in range(3)]
            prev[...] = jnp.concatenate(whole, axis=1)
            for (ref, g), x in zip(views, whole):
                ref[here, group(g)] = x
                if ref is winv:
                    for n, part in enumerate(split3(x)):
                        winv3[n, here, group(g)] = part
            return carry

        lax.fori_loop(0, LANE // BASE, body, 0, unroll=2)


def kernel(n_row, n_col, batch_axis, a_ref, share, diag, edge, stage, first, panel, work, winv, winv3, prev, fac, load_sem,
           seed_send, seed_recv, edge_send, edge_recv, first_sem, send_sem, pass_sem, down_sem, recv_sem):
    row_blocks, size, local_cols = a_ref.shape
    col_blocks = local_cols // size
    ratio = n_col // n_row
    steps = row_blocks * n_row
    depth = pass_sem.shape[0]
    batch = lax.axis_index(batch_axis)
    row = lax.axis_index("row")
    col = lax.axis_index("col")
    odd = lax.rem(col, 2)
    on_diag = lax.rem(col, n_row) == row
    row_slots = n_row * (row_blocks * (row_blocks + 1) // 2)
    edge_slots = row_slots + n_col * (col_blocks * (col_blocks + 1) // 2)
    leads = row == LEAD

    def at(dev_row, dev_col):
        return (batch, dev_row, dev_col)

    def row_slot(k, a):
        g = k // n_row
        return n_row * (row_blocks * g - (g * (g - 1)) // 2) + (k - g * n_row) * (row_blocks - g) + a - g

    def col_slot(k, b):
        h = k // n_col
        return row_slots + n_col * (col_blocks * h - (h * (h - 1)) // 2) + (k - h * n_col) * (col_blocks - h) + b - h

    def first_a(k):
        return (k + n_row - row) // n_row

    def first_b(k):
        return (k + n_col - col) // n_col

    def spot(a, b, count=1):
        return (a if count == 1 else pl.ds(a, count), slice(None), pl.ds(pl.multiple_of(b * size, size), size))

    def col_of(k, b):
        return jnp.where(on_diag, row_slot(k, ratio * b + col // n_row), col_slot(k, b))

    def edge_slot(k):
        return edge_slots + k

    def edge_reach(ahead):
        return jnp.logical_and(ahead >= 2, jnp.logical_and(ahead <= n_col + LAG - SETTLE, row != LEAD))

    def copy(src_slot, dst_slot, sem, device):
        return pltpu.make_async_remote_copy(
            src_ref=panel.at[src_slot], dst_ref=panel.at[dst_slot], send_sem=sem, recv_sem=recv_sem.at[dst_slot],
            device_id=device, device_id_type=MESH,
        )

    def arrived(slot):
        copy(slot, slot, send_sem.at[0, 0], at(row, col)).wait_recv()

    def start(c):
        c.start()

    def finish(c):
        c.wait_send()

    def from_maker(ahead, way):
        there = lax.rem(row + way, n_row)
        lead_near = jnp.logical_and(there == LEAD, jnp.logical_and(ahead >= 2, ahead <= n_row))
        soon_needed = jnp.logical_and(ahead == 2, way == 2)
        return jnp.logical_or(lead_near, soon_needed)

    def down_column(k, a, maker, sems, act):
        i = a * n_row + row
        slot = row_slot(k, a)
        dst = col_slot(k, i // n_col)
        for m, way in enumerate((1, n_row - 1, 2)):
            direct = from_maker(i - k, way)

            @pl.when(jnp.where(maker, direct, jnp.logical_not(direct)))
            def _():
                act(copy(slot, dst, sems[m], at(lax.rem(row + way, n_row), lax.rem(i, n_col))))

    def last_near(p):
        return first_a(p + 2)

    def to_edge(k, a, sem, act):
        i = a * n_row + row
        act(copy(row_slot(k, a), edge_slot(k), sem, at(LEAD, lax.rem(i - 1, n_col))))

    def source_sends(k, a, act):
        ahead = a * n_row + row - k
        slot = row_slot(k, a)
        early = n_row

        @pl.when(edge_reach(ahead))
        def _():
            to_edge(k, a, send_sem.at[a, 5], act)

        near = jnp.logical_and(ahead >= 2, ahead <= early)

        @pl.when(jnp.logical_or(near, lax.rem(ahead, n_col) == 0))
        def _():
            down_column(k, a, near, [send_sem.at[a, m] for m in range(3)], act)

        @pl.when(jnp.logical_or(jnp.logical_and(odd == 0, ahead >= 2), ahead >= n_col - 1))
        def _():
            act(copy(slot, slot, send_sem.at[a, 3], at(row, lax.rem(jnp.where(odd == 0, col + 1, col - 1), n_col))))

        @pl.when(ahead >= 2)
        def _():
            act(copy(slot, slot, send_sem.at[a, 6], at(row, lax.rem(col - odd + 2, n_col))))

        @pl.when(jnp.logical_and(ahead >= 3 - odd, a <= last_near(k)))
        def _():
            act(copy(slot, slot, send_sem.at[a, 4], at(row, lax.rem(col - odd + 3, n_col))))

        @pl.when(jnp.logical_and(ahead >= n_col // 2 - odd, ahead < n_col - 2 - odd))
        def _():
            act(copy(slot, slot, send_sem.at[a, 7], at(row, lax.rem(col - odd + 5, n_col))))

        @pl.when(ahead >= n_col - 2 - odd)
        def _():
            act(copy(slot, slot, send_sem.at[a, 8], at(row, lax.rem(col - odd - 2 + n_col, n_col))))

    def lead(p):
        return lax.rem(col - lax.rem(p, n_col) + n_col, n_col)

    def hops(p):
        return lax.rem(col // 2 - lax.rem(p, n_col) // 2 + n_col // 2, n_col // 2)

    def passes(p):
        return jnp.where(odd == 1, 2, n_col // 2 - 1) == hops(p)

    def first_passed(p):
        low = jnp.where(jnp.logical_and(passes(p), odd == 1), lead(p) - 1, lead(p))
        return (p + low - row + n_row - 1) // n_row

    def pass_down(p, a, act):
        i = a * n_row + row
        ahead = i - p
        sems = pass_sem.at[lax.rem(p, depth), a]

        @pl.when(jnp.logical_and(odd == 0, jnp.logical_and(lead(p) <= 2, a > last_near(p))))
        def _():
            act(copy(row_slot(p, a), row_slot(p, a), sems.at[0], at(row, col + 1)))

        @pl.when(jnp.logical_and(lax.rem(i, n_col) == col, ahead > 1))
        def _():
            downs = down_sem.at[lax.rem(p, depth), i // n_col]
            down_column(p, a, False, [downs.at[m] for m in range(3)], act)

    def pass_on(p, a, act):
        slot = row_slot(p, a)
        sems = pass_sem.at[lax.rem(p, depth), a]

        @pl.when(passes(p))
        def _():
            @pl.when(odd == 0)
            def _():
                act(copy(slot, slot, sems.at[1], at(row, lax.rem(col - 1 + n_col, n_col))))

            @pl.when(jnp.logical_or(odd == 1, a * n_row + row > p + lead(p)))
            def _():
                act(copy(slot, slot, sems.at[0], at(row, col + 1 - 2 * odd)))

        pass_down(p, a, act)

    def passed(p):
        @pl.when(lead(p) != 0)
        def _():
            loop(first_passed(p), row_blocks, lambda a: pass_on(p, a, finish))

    def receive(p, a):
        arrived(row_slot(p, a))
        pass_down(p, a, start)

    def receive_any(p, a):
        arrived(row_slot(p, a))
        pass_on(p, a, start)

    def loop(lo, hi, fn):
        lax.fori_loop(lo, hi, lambda n, c: (fn(n), c)[1], 0)

    load = pltpu.make_async_copy(a_ref, share, load_sem)
    load.start()

    barrier = pltpu.get_barrier_semaphore()
    n_dev = n_row * n_col

    def greet(n):
        other = lax.rem(row * n_col + col + n, n_dev)
        pl.semaphore_signal(barrier, inc=1, device_id=at(other // n_col, lax.rem(other, n_col)), device_id_type=MESH)

    loop(1, n_dev, greet)
    with jax.named_scope("all_here"):
        pl.semaphore_wait(barrier, n_dev - 1)
    with jax.named_scope("loaded"):
        load.wait()

    def seed_copy(b, dev_row):
        return pltpu.make_async_remote_copy(
            src_ref=share.at[spot(ratio * b + col // n_row, b)], dst_ref=diag.at[b],
            send_sem=seed_send.at[b, lax.rem(dev_row - row + n_row, n_row)],
            recv_sem=seed_recv.at[b], device_id=at(dev_row, col), device_id_type=MESH,
        )

    def hand_out(b):
        @pl.when(on_diag)
        def _():
            for d in (1, n_row - 1, 2):
                seed_copy(b, lax.rem(row + d, n_row)).start()
            diag[b] = share[spot(ratio * b + col // n_row, b)]

        @pl.when(jnp.logical_and(holds_edge(b), jnp.logical_not(leads)))
        def _():
            stage[b] = share[spot((b * n_col + col + 1) // n_row, b)]
            edge_copy(b).start()

    def holds_edge(b):
        j = b * n_col + col
        return jnp.logical_and(lax.rem(j + 1, n_row) == row, j + 1 < steps)

    def edge_copy(b):
        return pltpu.make_async_remote_copy(
            src_ref=stage.at[b], dst_ref=edge.at[b], send_sem=edge_send.at[b], recv_sem=edge_recv.at[b],
            device_id=at(LEAD, col), device_id_type=MESH,
        )

    def has_edge(b):
        from_other = jnp.logical_and(leads, lax.rem(col + 1, n_row) != LEAD)
        return jnp.logical_and(from_other, b * n_col + col + 1 < steps)

    def edge_seeded(b):
        @pl.when(has_edge(b))
        def _():
            edge_copy(b).wait_recv()

    def edge_arrived(p, b):
        j = b * n_col + col

        @pl.when(jnp.logical_and(has_edge(b), j + 1 - p <= n_col + LAG - SETTLE))
        def _():
            arrived(edge_slot(p))

    hand_out(0)
    winv3[...] = jnp.zeros(winv3.shape, BF16)

    def seed_arrived(b):
        @pl.when(jnp.logical_not(on_diag))
        def _():
            seed_copy(b, row).wait_recv()

    with jax.named_scope("seed"):
        seed_arrived(0)

        @pl.when(col != 0)
        def _():
            edge_seeded(0)

    def clear(n):
        a, b = lax.rem(n, row_blocks), n // row_blocks

        @pl.when(a * n_row + row < b * n_col + col)
        def _():
            share[spot(a, b)] = jnp.zeros((size, size), F32)

    loop(0, row_blocks * col_blocks, clear)

    def times_t(x, y):
        return lax.dot_general(x, y, (((1,), (1,)), ((), ())), preferred_element_type=F32)

    def update_block(p, a, b):
        share[spot(a, b)] -= times_t(panel[row_slot(p, a)], panel[col_of(p, b)])

    def update_diag(p, b):
        other = panel[col_of(p, b)]
        diag[b] -= times_t(other, other)

    def update_edge(p, b):
        @pl.when(has_edge(b))
        def _():
            edge[b] -= times_t(panel[edge_slot(p)], panel[col_of(p, b)])

    def column_arrived(p, b):
        @pl.when(jnp.logical_not(on_diag))
        def _():
            arrived(col_slot(p, b))

    def update_column(p, b, lo):
        lone = lax.rem(row_blocks - lo, 2)

        @pl.when(lone == 1)
        def _():
            update_block(p, lo, b)

        def pair(m):
            a = lo + lone + 2 * m
            both = spot(a, b, 2)
            left = panel[pl.ds(row_slot(p, a), 2)].reshape(2 * size, size)
            share[both] -= times_t(left, panel[col_of(p, b)]).reshape(2, size, size)

        loop(0, (row_blocks - lo) // 2, pair)

    def trail(p, b_from, near):
        loop(b_from, col_blocks, lambda b: update_column(p, b, first_a(b * n_col + col - jnp.where(b == near, 0, 1))))

    def columns_arrived(p, b_from):
        def one(b):
            column_arrived(p, b)
            edge_arrived(p, b)

        loop(b_from, col_blocks, one)

    def prepare(b):
        prev[...] = jnp.zeros(prev.shape, F32)
        fac[...] = jnp.zeros(fac.shape, F32)
        work[size:, :] = jnp.zeros((BASE, size), F32)
        r_id = lax.broadcasted_iota(jnp.int32, (size + BASE, size), 0)
        c_id = lax.broadcasted_iota(jnp.int32, (size + BASE, size), 1)
        winv[...] = jnp.where(r_id == c_id, 1.0, 0.0).astype(F32)

    def times_winv_t(x):
        hi, mid, lo = split3(x)
        whi, wmid, wlo = winv3[0], winv3[1], winv3[2]
        small = times_t(lo, whi) + times_t(mid, wmid) + times_t(hi, wlo)
        return small + (times_t(mid, whi) + times_t(hi, wmid)) + times_t(hi, whi)

    def here_diag(k):
        return row == lax.rem(k, n_row)

    def solve(k, a, count):
        kb = k // n_col
        near = jnp.logical_and(a == first_a(k), jnp.logical_not(here_diag(k)))
        here = spot(a, kb, count)

        def shaped(x):
            return x if count == 1 else x.reshape(count, size, size)

        def apply(p):
            left = panel[pl.ds(row_slot(p, a), count)].reshape(count * size, size)
            share[here] -= shaped(times_t(left, panel[col_of(p, kb)]))

        @pl.when(jnp.logical_not(near))
        def _():
            for m in range(count):

                @pl.when(k >= 3)
                def _():
                    receive(k - 3, a + m)

                @pl.when(k >= 2)
                def _():
                    receive(k - 2, a + m)

            loop(jnp.maximum(k - 2 - LAG, 0), k - 1, apply)

        @pl.when(k > 0)
        def _():
            for m in range(count):
                receive(k - 1, a + m)
            apply(k - 1)

        x = times_winv_t(share[here].reshape(count * size, size))
        panel[pl.ds(row_slot(k, a), count)] = x.astype(BF16).reshape(count, size, size)
        share[here] = shaped(x)
        if count == 1:

            @pl.when(jnp.logical_and(near, jnp.logical_and(leads, lax.rem(k + 1, n_row) == LEAD)))
            def _():
                first[...] = panel[row_slot(k, a)]
                first_out(k, start)

        if count == 1:
            source_sends(k, a, start)
        else:
            loop(a, a + count, lambda n: source_sends(k, n, start))

    def update_near(p, b):
        update_diag(p, b)
        update_edge(p, b)

    def first_slot(k, dev_row):
        return jnp.where(lax.rem(k + 1, n_row) == dev_row, row_slot(k, (k + 1) // n_row), col_slot(k, (k + 1) // n_col))

    def first_copy(k, dev_row, sem):
        dst = first_slot(k, dev_row)
        return pltpu.make_async_remote_copy(
            src_ref=first, dst_ref=panel.at[dst], send_sem=sem, recv_sem=recv_sem.at[dst],
            device_id=at(dev_row, lax.rem(col + 1, n_col)), device_id_type=MESH,
        )

    def others_first(k, fn):
        urgent = lax.rem(k + 3, n_row)
        lone = urgent == LEAD
        for m in range(n_row - 1):
            fn(m, lax.rem(jnp.where(lone, LEAD + 1, urgent) + m + jnp.where(lax.rem(jnp.where(lone, LEAD + 1, urgent) - LEAD + n_row, n_row) + m >= n_row, 1, 0), n_row))

    def first_out(k, act):
        act(first_copy(k, LEAD, first_sem.at[0, 0]))

        @pl.when(odd == 0)
        def _():
            others_first(k, lambda m, r: act(first_copy(k, r, first_sem.at[0, 1 + m])))

    def first_down(k, act):
        @pl.when(odd == 0)
        def _():
            others_first(k, lambda m, r: act(copy(first_slot(k, LEAD), first_slot(k, r), first_sem.at[1, 1 + m], at(r, col))))

    def firsts_done(k):
        @pl.when(jnp.logical_and(leads, k + 1 < steps))
        def _():
            first_out(k, finish)

        @pl.when(jnp.logical_and(leads, k > 0))
        def _():
            first_down(k - 1, finish)

    @pl.when(col == 0)
    def _():
        prepare(0)
        work[0:size, :] = diag[0]

    def step(k):
        mine = jnp.logical_and(col == lax.rem(k, n_col), k < steps)
        kb = k // n_col
        last = k - 1
        soon = jnp.logical_and(col == lax.rem(k + 1, n_col), k + 1 < steps)

        @pl.when(mine)
        def _():
            with jax.named_scope("factor"):
                factor_block(work, winv, winv3, prev, fac)

            @pl.when(has_edge(kb))
            def _():
                with jax.named_scope("lead"):

                    @pl.when(k == 0)
                    def _():
                        edge_seeded(kb)

                    @pl.when(k > 0)
                    def _():
                        edge_arrived(last, kb)
                        update_edge(last, kb)

                    first[...] = times_winv_t(edge[kb]).astype(BF16)
                    first_out(k, start)

            lo = first_a(k)
            second = jnp.minimum(lo + 1, row_blocks)
            third = second + lax.rem(row_blocks - second, 2)
            with jax.named_scope("solve_near"):
                loop(lo, third, lambda a: solve(k, a, 1))
            with jax.named_scope("solve_two"):
                loop(0, (row_blocks - third) // 2, lambda m: solve(k, third + 2 * m, 2))

        @pl.when(k >= depth)
        def _():
            with jax.named_scope("passed"):
                passed(k - depth)

        @pl.when(mine)
        def _():
            @pl.when(row == lax.rem(k, n_row))
            def _():
                for d in range(1, n_row):
                    seed_copy(kb, lax.rem(row + d, n_row)).wait_send()
                r_id = lax.broadcasted_iota(jnp.int32, (size, size), 0)
                c_id = lax.broadcasted_iota(jnp.int32, (size, size), 1)
                share[spot(k // n_row, kb)] = jnp.where(r_id >= c_id, work[0:size, :].T, 0.0)

        @pl.when(jnp.logical_and(k > 0, jnp.logical_not(jnp.logical_or(mine, soon))))
        def _():
            @pl.when(col != lax.rem(last, n_col))
            def _():
                with jax.named_scope("receive"):
                    end = jnp.where(lead(last) == 3, jnp.minimum(last_near(last) + 1, row_blocks), row_blocks)
                    loop(first_passed(last), end, lambda a: receive_any(last, a))

            near = first_b(k)
            age = k + n_col - (near * n_col + col)
            settle = jnp.logical_and(age == SETTLE, jnp.logical_and(near > 0, near < col_blocks))

            @pl.when(settle)
            def _():
                with jax.named_scope("late_trail"):
                    own = k - SETTLE

                    for back in (LAG + 2, LAG + 1, LAG):

                        @pl.when(own >= back)
                        def _():
                            columns_arrived(own - back, near)

                    loop(jnp.maximum(own - 2 - LAG, 0), own - LAG + 1, lambda p: trail(p, near, -1))

            @pl.when(jnp.logical_and(k >= LAG, lead(last) != 3))
            def _():
                p = k - LAG
                with jax.named_scope("columns"):
                    columns_arrived(p, near)

                @pl.when(jnp.logical_and(near < col_blocks, age >= SETTLE + 2))
                def _():
                    @pl.when(jnp.logical_and(age == SETTLE + 2, near > 0))
                    def _():
                        with jax.named_scope("seed_late"):
                            seed_arrived(near)
                            edge_seeded(near)

                    oldest = jnp.where(age == SETTLE + 2, jnp.maximum(p - 1, 0), p)
                    loop(oldest, p + 1, lambda q: update_near(q, near))

                with jax.named_scope("trail"):
                    trail(p, near, jnp.where(jnp.logical_or(age > SETTLE, near == 0), near, -1))

            @pl.when(settle)
            def _():
                hand_out(near)

        @pl.when(soon)
        def _():
            nb = (k + 1) // n_col

            oldest = jnp.maximum(k - 1 - LAG, 0)
            lo = first_a(k + 1)

            def old_diag(p):
                column_arrived(p, nb)
                edge_arrived(p, nb)
                update_near(p, nb)

            def take(a):
                receive(last, a)

                @pl.when(jnp.logical_not(here_diag(k + 1)))
                def _():
                    loop(oldest, last, lambda p: update_block(p, a, nb))

            @pl.when(k > 0)
            def _():
                with jax.named_scope("old_diag"):
                    loop(oldest, last, old_diag)
                with jax.named_scope("take"):
                    loop(first_a(k), jnp.minimum(first_a(k) + 1, row_blocks), take)
                with jax.named_scope("take_column"):
                    column_arrived(last, nb)
                    edge_arrived(last, nb)
                with jax.named_scope("catch_up"):
                    update_near(last, nb)
                    @pl.when(jnp.logical_and(jnp.logical_not(here_diag(k + 1)), lo < row_blocks))
                    def _():
                        update_block(last, lo, nb)

            prepare(nb)
            slot = col_of(k, nb)
            with jax.named_scope("first_block"):
                arrived(slot)

            @pl.when(leads)
            def _():
                first_down(k, start)

            other = panel[slot]
            work[0:size, :] = diag[nb] - times_t(other, other)

        @pl.when(jnp.logical_and(k >= n_col // 2, col == lax.rem(k + n_col // 2, n_col)))
        def _():
            with jax.named_scope("sends_done"):
                firsts_done(k - n_col // 2)
                loop(first_a(k - n_col // 2), row_blocks, lambda a: source_sends(k - n_col // 2, a, finish))

    loop(0, steps + n_col // 2, step)

    def edges_done(b):
        @pl.when(jnp.logical_and(holds_edge(b), jnp.logical_not(leads)))
        def _():
            edge_copy(b).wait_send()

    loop(0, col_blocks, edges_done)


def solution(mesh):
    n_row = mesh.shape["row"]
    n_col = mesh.shape["col"]

    def factor_local(a_loc):
        row_blocks, size, local_cols = a_loc.shape
        col_blocks = local_cols // size
        slots = n_row * (row_blocks * (row_blocks + 1) // 2) + n_col * (col_blocks * (col_blocks + 1) // 2)
        slots += row_blocks * n_row
        return pl.pallas_call(
            functools.partial(kernel, n_row, n_col, "batch"),
            out_shape=pltpu.VMEM(a_loc.shape, F32),
            in_specs=[pl.BlockSpec(memory_space=pl.ANY)],
            scratch_shapes=[
                pltpu.VMEM((col_blocks, size, size), F32),
                pltpu.VMEM((col_blocks, size, size), F32),
                pltpu.VMEM((col_blocks, size, size), F32),
                pltpu.VMEM((size, size), BF16),
                pltpu.VMEM((slots, size, size), BF16),
                pltpu.VMEM((size + BASE, size), F32),
                pltpu.VMEM((size + BASE, size), F32),
                pltpu.VMEM((3, size, size), BF16),
                pltpu.VMEM((BASE, 3 * LANE), F32),
                pltpu.VMEM((4 * SUB, SUB, LANE), F32),
                pltpu.SemaphoreType.DMA,
                pltpu.SemaphoreType.DMA((col_blocks, n_row)),
                pltpu.SemaphoreType.DMA((col_blocks,)),
                pltpu.SemaphoreType.DMA((col_blocks,)),
                pltpu.SemaphoreType.DMA((col_blocks,)),
                pltpu.SemaphoreType.DMA((2, n_row)),
                pltpu.SemaphoreType.DMA((row_blocks, 9)),
                pltpu.SemaphoreType.DMA((4, row_blocks, 2)),
                pltpu.SemaphoreType.DMA((4, col_blocks, 3)),
                pltpu.SemaphoreType.DMA((slots,)),
            ],
            compiler_params=pltpu.CompilerParams(
                collective_id=0, has_side_effects=True, vmem_limit_bytes=50 * 1024 * 1024
            ),
            name="cholesky",
        )(a_loc)

    blk_spec = P(("batch", "row"), None, "col")
    return jax.shard_map(factor_local, mesh=mesh, in_specs=(blk_spec,), out_specs=blk_spec, check_vma=False)
```

profile of v0, /device:TPU:103, one launch (start us, length us, event | category | flops | bytes accessed | tf_op | source)
XLA Modules:
  0.0 354.5 jit_solution(17618612221750026430)
XLA Ops:
  0.0 351.1 %cholesky.1 = f32[8,256,1024]{2,1,0:T(8,128)S(1)} custom-call(f32[8,256,1024]{2,1,0:T(8,128)} %a_ref.1), custom_call_target="tpu_custom_call" | custom-call | tf_op jit(solution)/shard_map/cholesky/pallas_call | solution.py:751
  351.1 3.4 copy.3
where the time goes:
time: 355 us; the launch traced here: 354 us
  Pallas kernels  351 us (99%)
    pallas_call x1, Pallas kernels, factor_local(): pl.pallas_call(functools.partial(kernel, n_row, n_col, 'batch'), out_shap...  351 us

commit v1 on v0

--- a/solution.py
+++ b/solution.py
@@ -13,7 +13,7 @@
 SUB = 8
 LANE = 128
 BASE = 16
-LEAD = 1
+LEAD = 3
 SETTLE = 3
 LAG = 3
 

time: 355 us -> 359 us (1.011)
  Pallas kernels: 351 us -> 355 us
    pallas_call x1, Pallas kernels: 351 us -> 355 us  [factor_local(): pl.pallas_call(functools.partial(kernel, n_row, n_col, 'batch'), out_shap...]
where the time goes in v1:
time: 359 us
  Pallas kernels  355 us (99%)
    pallas_call x1, Pallas kernels, factor_local(): pl.pallas_call(functools.partial(kernel, n_row, n_col, 'batch'), out_shap...  355 us

profile of v1, /device:TPU:103, one launch (start us, length us, event | category | flops | bytes accessed | tf_op | source)
XLA Modules:
  0.0 358.9 jit_solution(10829883322624689551)
XLA Ops:
  0.0 355.4 %cholesky.1 = f32[8,256,1024]{2,1,0:T(8,128)S(1)} custom-call(f32[8,256,1024]{2,1,0:T(8,128)} %a_ref.1), custom_call_target="tpu_custom_call" | custom-call | tf_op jit(solution)/shard_map/cholesky/pallas_call | solution.py:751
  355.5 3.4 copy.3
